TPU v7x, 32 devices: a whole 2x2x4 slice. The times are simulated.
32 devices in a mesh: seq: 8 (over z, core), tp: 4 (over y, x).
Axes of the slice: x: 2, y: 2, z: 4, core: 2. Of those that a mesh axis runs over, the one named last changes fastest.
Arguments:
- tokens: bfloat16 [2048, 4608], P('seq', 'tp'), may hold values from -6 to 6
- attention_gain: float32 [4608], replicated, may hold values from 0.25 to 1.75
- query_weight: bfloat16 [4608, 4096], P(None, 'tp'), may hold values from -0.09375 to 0.09375
- key_weight: bfloat16 [4608, 2048], P(None, 'tp'), may hold values from -0.09375 to 0.09375
- value_weight: bfloat16 [4608, 2048], P(None, 'tp'), may hold values from -0.09375 to 0.09375
- output_weight: bfloat16 [4096, 4608], P('tp'), may hold values from -0.09375 to 0.09375
- post_gain: float32 [4608], replicated, may hold values from 0.25 to 1.75
- local_gain: float32 [4608], replicated, may hold values from 0.25 to 1.75
- local_query_weight: bfloat16 [4608, 4096], P(None, 'tp'), may hold values from -0.09375 to 0.09375
- local_key_weight: bfloat16 [4608, 2048], P(None, 'tp'), may hold values from -0.09375 to 0.09375
- local_value_weight: bfloat16 [4608, 2048], P(None, 'tp'), may hold values from -0.09375 to 0.09375
Outputs:
- hidden: bfloat16 [2048, 4608], P('seq', 'tp')
- local_heads: bfloat16 [2048, 4096], P('seq', 'tp')
All inputs are finite; a program needn't handle non-finite values.
Results may differ from a plain program's by a relative error of at most 0.02.
Values may be sent and summed in bfloat16 or wider, within the bound.
A program may use at most 128 MiB of HBM per device.

v0:
```python
import jax
import jax.numpy as jnp
from jax import lax
from jax.sharding import PartitionSpec as P

D = 4608
HEADS = 32
HEAD_DIM = 128


SOFT_CAP = 50.0
NORM_EPS = 1e-06


def passed_along(value, axis, steps):
    count = lax.axis_size(axis)
    leading, last = (max(0, -steps), min(count, count - steps))
    return lax.ppermute(value, axis, [(source, source + steps) for source in range(leading, last)])


def rms_scaled(values, weights):
    widened = values.astype(jnp.float32)
    factor = lax.rsqrt(jnp.mean(widened * widened, axis=-1, keepdims=True) + NORM_EPS)
    return widened * factor * weights


def rotate(vectors, places):
    head_size = vectors.shape[-1]
    halfway = head_size // 2
    exponents = jnp.arange(halfway, dtype=jnp.float32) * (2.0 / head_size)
    frequency = jnp.power(jnp.float32(10000.0), -exponents)
    angles = places.astype(jnp.float32)[:, None] * frequency[None, :]
    cosine_part = jnp.cos(angles)[:, None, :]
    sine_part = jnp.sin(angles)[:, None, :]
    first_half = vectors[..., :halfway]
    second_half = vectors[..., halfway:]
    return jnp.concatenate(
        [
            first_half * cosine_part - second_half * sine_part,
            second_half * cosine_part + first_half * sine_part,
        ],
        axis=-1,
    )


def project_heads(normed, weight_query, weight_key, weight_value, places):
    row_count = normed.shape[0]
    queries = jnp.dot(normed, weight_query, preferred_element_type=jnp.float32).reshape(
        row_count, -1, HEAD_DIM
    )
    key_heads = jnp.dot(normed, weight_key, preferred_element_type=jnp.float32).reshape(
        row_count, -1, HEAD_DIM
    )
    value_heads = jnp.dot(normed, weight_value, preferred_element_type=jnp.float32).reshape(
        row_count, -1, HEAD_DIM
    )
    return (
        rotate(queries, places).astype(jnp.bfloat16),
        rotate(key_heads, places).astype(jnp.bfloat16),
        value_heads.astype(jnp.bfloat16),
    )


def empty_carry(queries, kv_heads):
    row_count = queries.shape[0]
    groups = queries.shape[1] // kv_heads
    return (
        jnp.zeros((row_count, kv_heads, groups, HEAD_DIM), jnp.float32),
        jnp.zeros((kv_heads, groups, row_count), jnp.float32),
    )


def attend_block(queries, query_places, key_block, value_block, key_places, window_size):
    kv_heads = key_block.shape[1]
    groups = queries.shape[1] // kv_heads
    grouped = queries.reshape(queries.shape[0], kv_heads, groups, queries.shape[2])
    scale = float(D // HEADS) ** (-0.5)
    scores = (
        jnp.einsum("qhrd,khd->hrqk", grouped, key_block, preferred_element_type=jnp.float32) * scale
    )
    scores = SOFT_CAP * jnp.tanh(scores / SOFT_CAP)
    offset = query_places[:, None] - key_places[None, :]
    allowed = (offset >= 0) & (key_places >= 0)[None, :]
    if window_size is not None:
        allowed = allowed & (offset < window_size)
    weights = jnp.where(allowed[None, None], jnp.exp(scores), jnp.float32(0.0))
    denominator = jnp.sum(weights, axis=-1)
    numerator = jnp.einsum(
        "hrqk,khd->qhrd",
        weights.astype(jnp.bfloat16),
        value_block,
        preferred_element_type=jnp.float32,
    )
    return (numerator, denominator)


def finish_heads(running):
    numerator, denominator = running
    averaged = numerator / jnp.transpose(denominator, (2, 0, 1))[..., None]
    return averaged.astype(jnp.bfloat16).reshape(numerator.shape[0], -1)


def visit_one(partial_sum, query_set, key_block, value_block, key_places, needed):

    def compute(current):
        return attend_block(query_set[0], query_set[1], key_block, value_block, key_places, None)

    return lax.cond(needed, compute, lambda current: current, partial_sum)


def causal_sets(query_sets, key_heads, value_heads):
    kv_heads = key_heads.shape[1]
    initial = tuple((empty_carry(query_set[0], kv_heads) for query_set in query_sets))
    latest = tuple((jnp.max(query_set[1]) for query_set in query_sets))
    first_row = jnp.int32(0)
    key_block = lax.all_gather(key_heads, "seq", axis=0, tiled=True)
    value_block = lax.all_gather(value_heads, "seq", axis=0, tiled=True)
    key_places = lax.iota(jnp.int32, key_block.shape[0])
    updated = []
    for query_set, visit_partial_sum, newest in zip(query_sets, initial, latest):
        updated.append(
            visit_one(
                visit_partial_sum,
                query_set,
                key_block,
                value_block,
                key_places,
                first_row <= newest,
            )
        )
    totals = tuple(updated)
    return [finish_heads(partial_sum) for partial_sum in totals]


def local(
    tokens,
    attention_gain,
    query_weight,
    key_weight,
    value_weight,
    output_weight,
    post_gain,
    local_gain,
    local_query_weight,
    local_key_weight,
    local_value_weight,
):
    row_count = tokens.shape[0]
    column_count = tokens.shape[1]
    section_index = lax.axis_index("seq")
    places = section_index * row_count + lax.iota(jnp.int32, row_count)
    full_rows = lax.all_gather(tokens, "tp", axis=1, tiled=True)
    normed = rms_scaled(full_rows, attention_gain).astype(jnp.bfloat16)
    queries, key_heads, value_heads = project_heads(
        normed, query_weight, key_weight, value_weight, places
    )
    attended = causal_sets([(queries, places)], key_heads, value_heads)[0]
    summed = lax.psum(
        jnp.dot(attended, output_weight, preferred_element_type=jnp.float32).astype(jnp.bfloat16),
        "tp",
    ).astype(jnp.float32)
    whole_hidden = (full_rows.astype(jnp.float32) + rms_scaled(summed, post_gain)).astype(
        jnp.bfloat16
    )
    hidden = lax.dynamic_slice_in_dim(
        whole_hidden, lax.axis_index("tp") * column_count, column_count, 1
    )
    local_normed = rms_scaled(whole_hidden, local_gain).astype(jnp.bfloat16)
    local_queries, local_keys, local_values = project_heads(
        local_normed, local_query_weight, local_key_weight, local_value_weight, places
    )
    window_size = row_count // 2
    tails = jnp.stack(
        [local_keys[row_count - window_size :], local_values[row_count - window_size :]]
    )
    earlier = passed_along(tails, "seq", 1)
    key_block = jnp.concatenate([earlier[0], local_keys], axis=0)
    value_block = jnp.concatenate([earlier[1], local_values], axis=0)
    key_places = (
        section_index * row_count - window_size + lax.iota(jnp.int32, window_size + row_count)
    )
    result = attend_block(local_queries, places, key_block, value_block, key_places, window_size)
    local_heads = finish_heads(result)
    return (hidden, local_heads)


def solution(mesh):
    in_specs = (
        P("seq", "tp"),
        P(),
        P(None, "tp"),
        P(None, "tp"),
        P(None, "tp"),
        P("tp", None),
        P(),
        P(),
        P(None, "tp"),
        P(None, "tp"),
        P(None, "tp"),
    )
    out_specs = (P("seq", "tp"), P("seq", "tp"))
    return jax.shard_map(local, mesh=mesh, in_specs=in_specs, out_specs=out_specs, check_vma=False)
```

profile of v0, /device:TPU:24, one launch (start us, length us, event | category | flops | bytes accessed | tf_op | source)
XLA Modules:
  0.0 259.5 jit_solution(231217193242092318)
XLA Ops:
  9.2 39.0 %all-gather.4.cloned.1.call-done = bf16[256,4608]{1,0:T(8,128)(2,1)} async-done(((bf16[256,1152]{1,0:T(8,128)(2,1)}), bf16[256,4608]{1,0:T(8,128)(2,1)}) %all-gather.4.cloned.1.call-update) | async-done | bytes 2359312 | tf_op jit(solution)/shard_map/all_gather | solution.py:152
  48.2 2.2 fusion.22
  50.4 5.3 %fusion.58 = f32[256,512]{1,0:T(8,128)} fusion(bf16[4608,512]{1,0:T(8,128)(2,1)} %param.16, bf16[256,4608]{1,0:T(8,128)(2,1)} %all-gather.4.cloned.1.call-done, f32[4608]{0:T(1024)} %param.14, f32[256]{0:T(256)S(1)} %add_rsqrt_fusion.2), kind=kOutput, calls=%fused_computation.94 | convolution fusion | flops 1212678144 | bytes 7621632 | tf_op jit(solution)/shard_map/dot_general | solution.py:51
  55.7 1.4 reshape.222
  57.5 0.9 pad_maximum_fusion.1
  58.5 3.8 %fusion.34 = bf16[32,4,8,128]{3,2,1,0:T(8,128)(2,1)S(1)} fusion(bf16[4608,512]{1,0:T(8,128)(2,1)} %param.17, bf16[256,4608]{1,0:T(8,128)(2,1)S(1)} %copy-done, f32[4608]{0:T(1024)S(1)} %copy-done.15, f32[256]{0:T(256)S(1)} %add_rsqrt_fusion.2), kind=kOutput, calls=%fused_computation.42 | convolution fusion | flops 1212809216 | bytes 7359488 | tf_op jit(solution)/shard_map/dot_general | solution.py:54
  64.3 5.6 %convolution_bitcast_fusion.1 = f32[32,8,8,128]{3,1,2,0:T(8,128)S(1)} fusion(bf16[4608,1024]{1,0:T(8,128)(2,1)} %param.15, bf16[256,4608]{1,0:T(8,128)(2,1)S(1)} %copy-done, f32[4608]{0:T(1024)S(1)} %copy-done.15, f32[256]{0:T(256)S(1)} %add_rsqrt_fusion.2), kind=kOutput, calls=%fused_computation.38 | convolution fusion | flops 2420637696 | bytes 12864512 | tf_op jit(solution)/shard_map/dot_general | solution.py:48
  70.8 1.1 pad_maximum_fusion
  71.9 14.3 %all-gather.6.cloned.1.call-done = bf16[2048,4,128]{2,0,1:T(8,128)(2,1)} async-done(((bf16[256,4,128]{2,0,1:T(8,128)(2,1)}), bf16[2048,4,128]{2,0,1:T(8,128)(2,1)}) %all-gather.6.cloned.1.call-update) | async-done | bytes 2097168 | tf_op jit(solution)/shard_map/all_gather | solution.py:116
  86.2 30.2 %all-gather.8.cloned.1.call-done = bf16[2048,4,128]{2,0,1:T(8,128)(2,1)} async-done(((bf16[256,4,128]{2,0,1:T(8,128)(2,1)}), bf16[2048,4,128]{2,0,1:T(8,128)(2,1)}) %all-gather.8.cloned.1.call-update) | async-done | bytes 2097168 | tf_op jit(solution)/shard_map/all_gather | solution.py:117
  116.4 17.3 %conditional.1 = (f32[4,2,256]{2,1,0:T(2,128)S(1)}, f32[256,4,2,128]{0,3,2,1:T(8,128)S(1)}) conditional(s32[]{:T(128)} %convert_element_type.65, () %tuple.16, (s32[256]{0:T(256)}, s32[2048]{0:T(1024)S(1)}, s32[2048]{0:T(1024)S(1)}, bf16[256,8,128]{2,0,1:T(8,128)(2,1)}, bf16[2048,4,128]{2,0,1:T(8,128)(2,1)}, ...), branch_computations={%region_2.0_spmd, %region_3.5_spmd} | conditional | flops 2182610944 | bytes 51409964 | solution.py:108
  116.4 2.2 fusion.8
  118.6 6.8 %fusion = (f32[4,2,256]{2,1,0:T(2,128)S(1)}, f32[4,2048,256,2]{2,1,3,0:T(8,128)S(1)}) fusion(pred[256,2048]{0,1:T(8,128)(4,1)S(1)} %fusion.8, bf16[256,4,2,128]{3,0,2,1:T(8,128)(2,1)} %bitcast.90, bf16[2048,4,128]{2,0,1:T(8,128)(2,1)} %get-tuple-element.14), kind=kOutput, calls=%fused_computation.1 | convolution fusion | flops 1090516992 | bytes 19931136 | tf_op jit(solution)/shard_map/cond/branch_1_fun/qhrd,khd->hrqk/dot_general | solution.py:79
  125.4 6.5 %fusion.9 = f32[256,4,2,128]{3,0,2,1:T(8,128)} fusion(bf16[2048,4,128]{2,0,1:T(8,128)(2,1)S(1)} %copy-done.14, f32[4,2048,256,2]{2,1,3,0:T(8,128)S(1)} %get-tuple-element.31, pred[256,2048]{0,1:T(8,128)(4,1)S(1)} %fusion.8), kind=kOutput, calls=%fused_computation.10 | convolution fusion | flops 1090519040 | bytes 20447232 | tf_op jit(solution)/shard_map/cond/branch_1_fun/hrqk,khd->qhrd/dot_general | solution.py:88
  131.9 1.6 copy.52
  133.8 7.6 %convolution_convert_fusion = bf16[256,4608]{1,0:T(8,128)(2,1)} fusion(bf16[256,1024]{0,1:T(8,128)(2,1)S(1)} %bitcast.88, bf16[1024,4608]{1,0:T(8,128)(2,1)} %param.18), kind=kOutput, calls=%fused_computation.18 | convolution fusion | flops 2417098752 | bytes 12320768 | tf_op jit(solution)/shard_map/dot_general | solution.py:159
  141.5 0.9 fusion.48
  142.4 74.0 %all-reduce.2.cloned.1.call-done = bf16[256,4608]{1,0:T(8,128)(2,1)} async-done(((bf16[256,4608]{1,0:T(8,128)(2,1)}), bf16[256,4608]{1,0:T(8,128)(2,1)}) %all-reduce.2.cloned.1.call-update) | async-done | bytes 2359312 | tf_op jit(solution)/shard_map/psum | solution.py:158
  216.4 2.2 fusion.17
  218.6 3.2 %fusion.19 = (f32[256]{0:T(256)S(1)}, bf16[256,4608]{1,0:T(8,128)(2,1)S(1)}) fusion(f32[4608]{0:T(1024)S(1)} %copy-done.12, f32[256]{0:T(256)S(1)} %add_rsqrt_fusion.1, bf16[256,4608]{1,0:T(8,128)(2,1)} %all-reduce.2.cloned.1.call-done, bf16[256,4608]{1,0:T(8,128)(2,1)S(1)} %copy-done), kind=kLoop, calls=%fused_computation.25 | loop fusion | flops 10616576 | bytes 7098368 | tf_op jit(solution)/shard_map/reduce_sum | solution.py:23
  221.9 6.1 %convolution_bitcast_fusion = f32[32,8,8,128]{3,1,2,0:T(8,128)S(1)} fusion(bf16[4608,1024]{1,0:T(8,128)(2,1)} %param.21, bf16[256,4608]{1,0:T(8,128)(2,1)S(1)} %get-tuple-element.29, f32[4608]{0:T(1024)S(1)} %copy-done.16, f32[256]{0:T(256)S(1)} %add_rsqrt_fusion), kind=kOutput, calls=%fused_computation.37 | convolution fusion | flops 2420637696 | bytes 12864512 | tf_op jit(solution)/shard_map/dot_general | solution.py:48
  228.6 1.4 fusion.63
  230.3 1.1 fusion.68
  231.4 4.5 %convolution_convert_fusion.1 = bf16[256,512]{1,0:T(8,128)(2,1)S(1)} fusion(bf16[4608,512]{1,0:T(8,128)(2,1)} %param.23, bf16[256,4608]{1,0:T(8,128)(2,1)} %copy-done.1, f32[4608]{0:T(1024)S(1)} %copy-done.17, f32[256]{0:T(256)S(1)} %add_rsqrt_fusion), kind=kOutput, calls=%fused_computation.40 | convolution fusion | flops 1212809216 | bytes 7359488 | tf_op jit(solution)/shard_map/dot_general | solution.py:54
  237.3 0.9 stack.10
  240.0 2.0 collective-permute-start
  242.1 1.4 subtract_convert_fusion
  243.6 1.9 constant_dynamic-slice_fusion
  245.5 2.5 collective-permute-done
  248.2 2.6 fusion.26
  250.8 1.1 divide_convert_fusion
  252.0 1.0 copy.43
  (78 shorter events, 9.2 us)
Async XLA Ops:
  7.2 41.0 %all-gather.4.cloned.1.call-start = ((), (), s32[]{:S(2)}) async-start(), calls=%async_computation | async-start | bytes 2949120 | tf_op jit(solution)/shard_map/all_gather | solution.py:152
  7.9 78.3 %all-gather.6.cloned.1.call-start = ((), (), s32[]{:S(2)}) async-start(), calls=%async_computation.1 | async-start | bytes 2359296 | tf_op jit(solution)/shard_map/all_gather | solution.py:116
  9.2 61.2 %copy-start.2 = (f32[256,64]{1,0:T(8,128)}, f32[256,64]{1,0:T(8,128)S(1)}, u32[]{:S(2)}) copy-start(f32[256,64]{1,0:T(8,128)S(1)} %get-tuple-element.51) | copy-start | bytes 196612
  55.7 2.8 %copy-start = (bf16[256,4608]{1,0:T(8,128)(2,1)S(1)}, bf16[256,4608]{1,0:T(8,128)(2,1)}, u32[]{:S(2)}) copy-start(bf16[256,4608]{1,0:T(8,128)(2,1)} %all-gather.4.cloned.1.call-done) | copy-start | bytes 7077892
  55.7 2.8 %copy-start.15 = (f32[4608]{0:T(1024)S(1)}, f32[4608]{0:T(1024)}, u32[]{:S(2)}) copy-start(f32[4608]{0:T(1024)} %param.14) | copy-start | bytes 55300
  58.4 58.0 %all-gather.8.cloned.1.call-start = ((), (), s32[]{:S(2)}) async-start(), calls=%async_computation.2 | async-start | bytes 2359296 | tf_op jit(solution)/shard_map/all_gather | solution.py:117
  63.0 153.3 %all-reduce.2.cloned.1.call-start = ((), (), s32[]{:S(2)}) async-start(), calls=%async_computation.3 | async-start | bytes 4718592 | tf_op jit(solution)/shard_map/psum | solution.py:158
  118.6 6.8 %copy-start.14 = (bf16[2048,4,128]{2,0,1:T(8,128)(2,1)S(1)}, bf16[2048,4,128]{2,0,1:T(8,128)(2,1)}, u32[]{:S(2)}) copy-start(bf16[2048,4,128]{2,0,1:T(8,128)(2,1)} %get-tuple-element.16) | copy-start | bytes 6291460 | tf_op jit(solution)/shard_map/cond
  133.8 7.7 %copy-start.13 = (s32[256]{0:T(256)S(1)}, s32[256]{0:T(256)}, u32[]{:S(2)}) copy-start(s32[256]{0:T(256)} %iota_add_fusion.1) | copy-start | bytes 3076
  141.5 77.2 %copy-start.12 = (f32[4608]{0:T(1024)S(1)}, f32[4608]{0:T(1024)}, u32[]{:S(2)}) copy-start(f32[4608]{0:T(1024)} %param.19) | copy-start | bytes 55300
  142.4 79.5 %copy-start.16 = (f32[4608]{0:T(1024)S(1)}, f32[4608]{0:T(1024)}, u32[]{:S(2)}) copy-start(f32[4608]{0:T(1024)} %param.20) | copy-start | bytes 55300
  218.6 10.0 %slice-start = ((s8[4718592]{0:T(1024)(128)(4,1)}), s8[4194304]{0:T(1024)(128)(4,1)S(1)}, s32[]{:S(2)}) async-start(s8[4718592]{0:T(1024)(128)(4,1)} %bitcast.96), calls=%async_computation.4 | async-start | bytes 8388608
  221.9 6.7 %copy-start.1 = (bf16[256,4608]{1,0:T(8,128)(2,1)}, bf16[256,4608]{1,0:T(8,128)(2,1)S(1)}, u32[]{:S(2)}) copy-start(bf16[256,4608]{1,0:T(8,128)(2,1)S(1)} %get-tuple-element.29) | copy-start | bytes 7077892
  221.9 6.7 %slice-start.1 = ((s8[4718592]{0:T(1024)(128)(4,1)}), s8[524288]{0:T(1024)(128)(4,1)S(1)}, s32[]{:S(2)}) async-start(s8[4718592]{0:T(1024)(128)(4,1)} %bitcast.96), calls=%async_computation.5 | async-start | bytes 1048576
  228.6 2.8 %copy-start.17 = (f32[4608]{0:T(1024)S(1)}, f32[4608]{0:T(1024)}, u32[]{:S(2)}) copy-start(f32[4608]{0:T(1024)} %param.20) | copy-start | bytes 55300
  231.4 6.9 %copy-start.3 = (f32[256,64]{1,0:T(8,128)S(1)}, f32[256,64]{1,0:T(8,128)}, u32[]{:S(2)}) copy-start(f32[256,64]{1,0:T(8,128)} %copy-done.2) | copy-start | bytes 196612
  231.4 6.9 %copy-start.4 = (f32[256,4,64]{2,1,0:T(4,128)S(1)}, f32[256,4,64]{2,1,0:T(4,128)}, u32[]{:S(2)}) copy-start(f32[256,4,64]{2,1,0:T(4,128)} %get-tuple-element.45) | copy-start | bytes 786436
  235.9 0.7 copy-start.9
  238.4 0.7 copy-start.5
  238.4 0.8 copy-start.7
  238.5 5.0 %copy-start.10 = (bf16[256,512]{1,0:T(8,128)(2,1)S(1)}, bf16[256,512]{1,0:T(8,128)(2,1)}, u32[]{:S(2)}) copy-start(bf16[256,512]{1,0:T(8,128)(2,1)} %copy-done.9) | copy-start | bytes 786436
  239.3 9.0 %copy-start.6 = (bf16[256,4,64]{2,0,1:T(8,128)(2,1)S(1)}, bf16[256,4,64]{2,0,1:T(8,128)(2,1)}, u32[]{:S(2)}) copy-start(bf16[256,4,64]{2,0,1:T(8,128)(2,1)} %copy-done.5) | copy-start | bytes 393220
  240.0 8.2 %copy-start.8 = (bf16[256,4,64]{2,0,1:T(8,128)(2,1)S(1)}, bf16[256,4,64]{2,0,1:T(8,128)(2,1)}, u32[]{:S(2)}) copy-start(bf16[256,4,64]{2,0,1:T(8,128)(2,1)} %copy-done.7) | copy-start | bytes 393220
  240.0 8.2 %copy-start.11 = (pred[256,384]{0,1:T(8,128)(4,1)S(1)}, pred[256,384]{0,1:T(8,128)(4,1)}, u32[]{:S(2)}) copy-start(pred[256,384]{0,1:T(8,128)(4,1)} %fusion.48) | copy-start | bytes 294916
  240.0 8.0 %collective-permute-start = (bf16[2,128,4,128]{3,1,2,0:T(8,128)(2,1)}, bf16[2,128,4,128]{3,1,2,0:T(8,128)(2,1)S(1)}, u32[]{:S(2)}, u32[]{:S(2)}) collective-permute-start(bf16[2,128,4,128]{3,1,2,0:T(8,128)(2,1)} %pad_maximum_fusion.2), channel_id=1, source_target_pairs={{0,4},{4,8},{8,12},{12,16},{16,20},{20,24},{24,28},{1,5},{5,9},{9,... | collective-permute-start | bytes 786440 | tf_op jit(solution)/shard_map/ppermute | solution.py:18
Sparse Core Ops, SparseCore 0:
  9.8 38.3 all-gather.3
  58.5 27.6 all-gather.5
  87.8 28.5 all-gather.7
  141.6 74.7 all-reduce.1
where the time goes:
time: 260 us; the launch traced here: 259 us
  waiting for transfers between devices  161 us (62%)
  matrix products  51.3 us (20%)
  other arithmetic  17.5 us (7%)
  between operations  14.8 us (6%)
  local copies, waits for them, and re-layouts  12.7 us (5%)
    psum x1, waiting for transfers between devices, local(): lax.psum(jnp.dot(attended, output_weight, preferred_element_type=jnp.floa...  74 us
    all_gather x1, waiting for transfers between devices, local(): full_rows = lax.all_gather(tokens, 'tp', axis=1, tiled=True)  39 us
    all_gather x1, waiting for transfers between devices, causal_sets(): value_block = lax.all_gather(value_heads, 'seq', axis=0, tiled=True)  30.2 us
    all_gather x1, waiting for transfers between devices, causal_sets(): key_block = lax.all_gather(key_heads, 'seq', axis=0, tiled=True)  14.3 us
    dot_general x2, matrix products, project_heads(): jnp.dot(normed, weight_query, preferred_element_type=jnp.float32)  11.7 us
    dot_general x2, matrix products, attend_block(): jnp.einsum('qhrd,khd->hrqk', grouped, key_block, preferred_element_type=j...  9.33 us
    dot_general x2, matrix products, project_heads(): jnp.dot(normed, weight_value, preferred_element_type=jnp.float32)  8.3 us
    dot_general x2, matrix products, attend_block(): jnp.einsum('hrqk,khd->qhrd', weights.astype(jnp.bfloat16), value_block, p...  7.66 us
  transfers between devices with their start and end apart: 5, of which 5 were waited for; matrix products, arithmetic and copies ran while one was open for 7% of the time, Pallas kernels for 0%

commit v1 on v0

v1 whole, which is shorter than its diff:
```python
import functools
import math

import jax
import jax.numpy as jnp
from jax import lax
from jax.experimental import pallas as pl
from jax.experimental.pallas import tpu as pltpu
from jax.sharding import PartitionSpec as P

D = 4608
HEADS = 32
HEAD_DIM = 128
WINDOW = 128

SOFT_CAP = 50.0
NORM_EPS = 1e-06
MESH = pl.DeviceIdType.MESH
VMEM = pltpu.VMEM
F32 = jnp.float32
BF16 = jnp.bfloat16
INNER = float(D // HEADS) ** (-0.5) / SOFT_CAP
OUTER = SOFT_CAP * math.log2(math.e)


def greet(peers):
    barrier = pltpu.get_barrier_semaphore()
    for peer in peers:
        pl.semaphore_signal(barrier, inc=1, device_id=peer, device_id_type=MESH)
    pl.semaphore_wait(barrier, len(peers))


def remote(source, target, send_sem, recv_sem, device):
    return pltpu.make_async_remote_copy(
        src_ref=source,
        dst_ref=target,
        send_sem=send_sem,
        recv_sem=recv_sem,
        device_id=device,
        device_id_type=MESH,
    )


def xor(index, bits):
    low, high = index % 2, index // 2
    if bits & 1:
        low = 1 - low
    if bits & 2:
        high = 1 - high
    return high * 2 + low


def gather_project_kernel(
    heads, kv_heads, x_ref, gain_ref, cos_ref, sin_ref, wq_ref, wk_ref, wv_ref,
    q_ref, kv_ref, buf, xg, w, acc, ss, send, recv, wsem,
):
    me = lax.axis_index("tp")
    rows, cols = x_ref.shape
    half = rows // 2
    owners = [xor(me, bits) for bits in range(4)]
    along_x, along_y = {"tp": owners[1]}, {"tp": owners[2]}
    qc, kc = heads * HEAD_DIM, kv_heads * HEAD_DIM
    total = qc + 2 * kc

    loads = []
    for slot in range(4):
        span = pl.ds(pl.multiple_of(owners[slot] * cols, cols), cols)
        parts = ((wq_ref, 0, qc), (wk_ref, qc, kc), (wv_ref, qc + kc, kc))
        group = []
        for which, (ref, begin, width) in enumerate(parts):
            copy = pltpu.make_async_copy(
                ref.at[span, :], w.at[slot, :, pl.ds(begin, width)], wsem.at[slot, which]
            )
            copy.start()
            group.append(copy)
        loads.append(group)

    greet([along_x, along_y])
    top, bottom = pl.ds(0, half), pl.ds(half, half)
    x_top = remote(x_ref.at[top], buf.at[0, top], send.at[0], recv.at[0], along_x)
    y_bottom = remote(x_ref.at[bottom], buf.at[1, bottom], send.at[1], recv.at[1], along_y)
    x_bottom = remote(x_ref.at[bottom], buf.at[0, bottom], send.at[2], recv.at[2], along_x)
    y_top = remote(x_ref.at[top], buf.at[1, top], send.at[3], recv.at[3], along_y)
    pass_y = remote(buf.at[0, top], buf.at[2, top], send.at[4], recv.at[4], along_y)
    pass_x = remote(buf.at[1, bottom], buf.at[2, bottom], send.at[5], recv.at[5], along_x)
    x_top.start()
    y_bottom.start()
    x_bottom.start()
    y_top.start()

    tile = 256 if total % 256 == 0 else 128
    step_rows = 64 if rows % 64 == 0 else rows

    def take(slot, source):
        gain_span = pl.ds(pl.multiple_of(owners[slot] * cols, cols), cols)

        def prepare(i, carry):
            part = pl.ds(pl.multiple_of(i * step_rows, step_rows), step_rows)
            wide = source[part, :].astype(F32)
            squares = jnp.sum(wide * wide, axis=-1, keepdims=True)
            spread = jnp.broadcast_to(squares, (step_rows, HEAD_DIM))
            if slot == 0:
                ss[part, :] = spread
            else:
                ss[part, :] += spread
            xg[part, :] = (wide * gain_ref[:, gain_span]).astype(BF16)
            return carry

        lax.fori_loop(0, rows // step_rows, prepare, 0)
        for copy in loads[slot]:
            copy.wait()

        def multiply(j, carry):
            span = pl.ds(pl.multiple_of(j * tile, tile), tile)
            product = jnp.dot(xg[...], w[slot, :, span], preferred_element_type=F32)
            if slot == 0:
                acc[:, span] = product
            else:
                acc[:, span] += product
            return carry

        lax.fori_loop(0, total // tile, multiply, 0)

    take(0, x_ref)
    x_top.wait_recv()
    pass_y.start()
    y_bottom.wait_recv()
    pass_x.start()
    x_bottom.wait_recv()
    take(1, buf.at[0])
    y_top.wait_recv()
    take(2, buf.at[1])
    pass_y.wait_recv()
    pass_x.wait_recv()
    take(3, buf.at[2])

    factor = lax.rsqrt(ss[...] * (1.0 / D) + NORM_EPS)

    def rotated(index):
        u = acc[:, pl.ds(index * HEAD_DIM, HEAD_DIM)] * factor
        return u * cos_ref[...] + pltpu.roll(u, HEAD_DIM // 2, 1) * sin_ref[...]

    for h in range(heads):
        q_ref[h] = rotated(h).astype(BF16)
    for h in range(kv_heads):
        kv_ref[0, h] = rotated(heads + h).astype(BF16)
        place = (heads + kv_heads + h) * HEAD_DIM
        kv_ref[1, h] = (acc[:, pl.ds(place, HEAD_DIM)] * factor).astype(BF16)
    for copy in (x_top, y_bottom, x_bottom, y_top, pass_y, pass_x):
        copy.wait_send()


def gather_project(x, gain, cos, sin, wq, wk, wv, collective_id):
    rows, cols = x.shape
    heads, kv_heads = wq.shape[1] // HEAD_DIM, wk.shape[1] // HEAD_DIM
    total = wq.shape[1] + 2 * wk.shape[1]
    vmem = pl.BlockSpec(memory_space=VMEM)
    hbm = pl.BlockSpec(memory_space=pl.ANY)
    return pl.pallas_call(
        functools.partial(gather_project_kernel, heads, kv_heads),
        out_shape=(
            jax.ShapeDtypeStruct((heads, rows, HEAD_DIM), BF16),
            jax.ShapeDtypeStruct((2, kv_heads, rows, HEAD_DIM), BF16),
        ),
        in_specs=[vmem] * 4 + [hbm] * 3,
        out_specs=(vmem, vmem),
        scratch_shapes=[
            VMEM((3, rows, cols), BF16),
            VMEM((rows, cols), BF16),
            VMEM((4, cols, total), BF16),
            VMEM((rows, total), F32),
            VMEM((rows, HEAD_DIM), F32),
            pltpu.SemaphoreType.DMA((6,)),
            pltpu.SemaphoreType.DMA((6,)),
            pltpu.SemaphoreType.DMA((4, 3)),
        ],
        compiler_params=pltpu.CompilerParams(
            collective_id=collective_id, has_side_effects=True, vmem_limit_bytes=48 * 2**20
        ),
        name=f"gather_project_{collective_id}",
    )(x, gain[None, :], cos, sin, wq, wk, wv)


def attend(q_ref, keys, values, acc, lsum, h, group, allowed, first, row_span=None):
    q = q_ref[pl.ds(h * group, group)]
    if row_span is not None:
        q = q[:, row_span[0] : row_span[1]]
    rows = q.shape[1]
    q = q.reshape(group * rows, HEAD_DIM)
    scores = lax.dot_general(q, keys, (((1,), (1,)), ((), ())), preferred_element_type=F32)
    weights = jnp.exp2(jnp.tanh(scores * INNER) * OUTER)
    if allowed is not None:
        count = keys.shape[0]
        row = lax.broadcasted_iota(jnp.int32, (rows, count), 0)
        col = lax.broadcasted_iota(jnp.int32, (rows, count), 1)
        mask = allowed(row, col)
        weights = jnp.concatenate(
            [jnp.where(mask, weights[g * rows : (g + 1) * rows], 0.0) for g in range(group)], axis=0
        )
    lanes = weights[:, :HEAD_DIM]
    for begin in range(HEAD_DIM, keys.shape[0], HEAD_DIM):
        lanes = lanes + weights[:, begin : begin + HEAD_DIM]
    product = jnp.dot(weights.astype(BF16), values, preferred_element_type=F32)
    lanes = lanes.reshape(group, rows, HEAD_DIM)
    product = product.reshape(group, rows, HEAD_DIM)
    heads = pl.ds(h * group, group)
    span = pl.ds(0, rows)
    if first:
        lsum[heads, span] = lanes
        acc[heads, span] = product
    else:
        lsum[heads, span] += lanes
        acc[heads, span] += product


def write_heads(o_ref, acc, lsum):
    for h in range(acc.shape[0]):
        denominator = jnp.sum(lsum[h], axis=-1, keepdims=True)
        o_ref[:, h * HEAD_DIM : (h + 1) * HEAD_DIM] = (acc[h] / denominator).astype(BF16)


def causal_kernel(levels, q_ref, kv_ref, o_ref, buf, acc, lsum, up_sem, side_sem, recv):
    s = lax.axis_index("seq")
    z, c = s // 2, s % 2
    mate = s + 1 - 2 * c
    kv_heads = kv_ref.shape[1]
    group = q_ref.shape[0] // kv_heads
    has_up, has_down = z < levels - 1, z > 0

    barrier = pltpu.get_barrier_semaphore()
    pl.semaphore_signal(barrier, inc=1, device_id={"seq": mate}, device_id_type=MESH)

    @pl.when(has_up)
    def _():
        pl.semaphore_signal(barrier, inc=1, device_id={"seq": s + 2}, device_id_type=MESH)

    @pl.when(has_down)
    def _():
        pl.semaphore_signal(barrier, inc=1, device_id={"seq": s - 2}, device_id_type=MESH)

    pl.semaphore_wait(barrier, 1 + has_up.astype(jnp.int32) + has_down.astype(jnp.int32))

    def up(owner, source):
        return remote(source, buf.at[owner], up_sem.at[owner], recv.at[owner], {"seq": s + 2})

    def side(owner, source):
        return remote(source, buf.at[owner], side_sem.at[owner], recv.at[owner], {"seq": mate})

    @pl.when(has_up)
    def _():
        up(s, kv_ref).start()

    @pl.when(c == 0)
    def _():
        side(s, kv_ref).start()

    def own(h, carry):
        attend(
            q_ref, kv_ref[0, h], kv_ref[1, h], acc, lsum, h, group,
            lambda row, col: col <= row, True,
        )
        return carry

    lax.fori_loop(0, kv_heads, own, 0)

    def visit(owner):
        def body(h, carry):
            attend(
                q_ref, buf[owner, 0, h], buf[owner, 1, h], acc, lsum, h, group, None, False
            )
            return carry

        lax.fori_loop(0, kv_heads, body, 0)

    @pl.when(c == 1)
    def _():
        side(s - 1, buf.at[s - 1]).wait_recv()
        visit(s - 1)

    def level(k, carry):
        owner, other = s - 2 * k, mate - 2 * k
        up(owner, buf.at[owner]).wait_recv()

        @pl.when(has_up)
        def _():
            up(owner, buf.at[owner]).start()

        side(owner, buf.at[owner]).start()
        visit(owner)
        side(other, buf.at[other]).wait_recv()
        visit(other)
        return carry

    lax.fori_loop(1, z + 1, level, 0)
    write_heads(o_ref, acc, lsum)

    @pl.when(has_up)
    def _():
        up(s, kv_ref).wait_send()

    @pl.when(c == 0)
    def _():
        side(s, kv_ref).wait_send()

    def drain(k, carry):
        owner = s - 2 * k

        @pl.when(has_up)
        def _():
            up(owner, buf.at[owner]).wait_send()

        side(owner, buf.at[owner]).wait_send()
        return carry

    lax.fori_loop(1, z + 1, drain, 0)


def causal_attention(q, kv, count, collective_id):
    heads, rows, _ = q.shape
    vmem = pl.BlockSpec(memory_space=VMEM)
    return pl.pallas_call(
        functools.partial(causal_kernel, count // 2),
        out_shape=jax.ShapeDtypeStruct((rows, heads * HEAD_DIM), BF16),
        in_specs=[vmem] * 2,
        out_specs=vmem,
        scratch_shapes=[
            VMEM((count,) + kv.shape, BF16),
            VMEM(q.shape, F32),
            VMEM(q.shape, F32),
            pltpu.SemaphoreType.DMA((count,)),
            pltpu.SemaphoreType.DMA((count,)),
            pltpu.SemaphoreType.DMA((count,)),
        ],
        compiler_params=pltpu.CompilerParams(
            collective_id=collective_id, has_side_effects=True, vmem_limit_bytes=32 * 2**20
        ),
        name="causal_attention",
    )(q, kv)


def output_kernel(
    a_ref, tok_ref, gain_ref, wo_ref, hidden_ref,
    wbuf, part, own, landed, passed, mine, stats, wsem, send, recv, ssend, srecv,
):
    me = lax.axis_index("tp")
    rows, cols = tok_ref.shape
    half = rows // 2
    owners = [xor(me, bits) for bits in range(4)]
    peers = [{"tp": owner} for owner in owners]
    order = (3, 1, 2, 0)
    loads = []
    for slot, bits in enumerate(order):
        span = pl.ds(pl.multiple_of(owners[bits] * cols, cols), cols)
        copy = pltpu.make_async_copy(wo_ref.at[:, span], wbuf.at[slot], wsem.at[slot])
        copy.start()
        loads.append(copy)
    greet(peers[1:])
    top, bottom = pl.ds(0, half), pl.ds(half, half)
    diag_x = remote(part.at[0, top], landed.at[0], send.at[0], recv.at[0], peers[1])
    diag_y = remote(part.at[0, bottom], landed.at[1], send.at[1], recv.at[1], peers[2])
    last_x_top = remote(part.at[1, top], landed.at[2], send.at[2], recv.at[2], peers[1])
    last_y_bottom = remote(part.at[2, bottom], landed.at[3], send.at[3], recv.at[3], peers[2])
    last_x_bottom = remote(passed.at[1], landed.at[4], send.at[4], recv.at[4], peers[1])
    last_y_top = remote(passed.at[0], landed.at[5], send.at[5], recv.at[5], peers[2])

    tile = 384 if cols % 384 == 0 else 128

    def product(slot, store):
        loads[slot].wait()

        def body(j, carry):
            span = pl.ds(pl.multiple_of(j * tile, tile), tile)
            store(span, jnp.dot(a_ref[...], wbuf[slot, :, span], preferred_element_type=F32))
            return carry

        lax.fori_loop(0, cols // tile, body, 0)

    def store_part(slot):
        def store(span, value):
            part[slot, :, span] = value.astype(BF16)

        return store

    def store_own(span, value):
        own[:, span] = value

    product(0, store_part(0))
    diag_x.start()
    diag_y.start()
    product(1, store_part(1))
    last_x_top.start()
    product(2, store_part(2))
    last_y_bottom.start()
    product(3, store_own)
    diag_x.wait_recv()
    passed[0] = (part[2, 0:half].astype(F32) + landed[0].astype(F32)).astype(BF16)
    last_y_top.start()
    diag_y.wait_recv()
    passed[1] = (part[1, half:rows].astype(F32) + landed[1].astype(F32)).astype(BF16)
    last_x_bottom.start()
    last_x_top.wait_recv()
    own[0:half] += landed[2].astype(F32)
    last_y_bottom.wait_recv()
    own[half:rows] += landed[3].astype(F32)
    last_y_top.wait_recv()
    own[0:half] += landed[5].astype(F32)
    last_x_bottom.wait_recv()
    own[half:rows] += landed[4].astype(F32)

    lanes = jnp.zeros((rows, HEAD_DIM), F32)
    for begin in range(0, cols, HEAD_DIM):
        piece = own[:, begin : begin + HEAD_DIM]
        lanes = lanes + piece * piece
    ones = jnp.ones((8, HEAD_DIM), F32)
    highest = lax.Precision.HIGHEST
    mine[...] = lax.dot_general(
        ones, lanes, (((1,), (1,)), ((), ())), precision=highest, preferred_element_type=F32
    )
    swaps = []
    for bits in (3, 1, 2):
        swap = remote(mine, stats.at[bits - 1], ssend.at[bits - 1], srecv.at[bits - 1], peers[bits])
        swap.start()
        swaps.append(swap)
    for swap in swaps:
        swap.wait_recv()
    summed = mine[...] + stats[0] + stats[1] + stats[2]
    column = lax.dot_general(
        summed, ones * 0.125, (((0,), (0,)), ((), ())), precision=highest,
        preferred_element_type=F32,
    )
    factor = lax.rsqrt(column * (1.0 / D) + NORM_EPS)
    span = pl.multiple_of(me * cols, cols)
    for begin in range(0, cols, HEAD_DIM):
        stop = begin + HEAD_DIM
        gain = gain_ref[:, pl.ds(pl.multiple_of(span + begin, HEAD_DIM), HEAD_DIM)]
        hidden_ref[:, begin:stop] = (
            tok_ref[:, begin:stop].astype(F32) + own[:, begin:stop] * factor * gain
        ).astype(BF16)
    for copy in (diag_x, diag_y, last_x_top, last_y_bottom, last_x_bottom, last_y_top, *swaps):
        copy.wait_send()


def output_project(attended, tokens, gain, wo, collective_id):
    rows, cols = tokens.shape
    depth = attended.shape[1]
    vmem = pl.BlockSpec(memory_space=VMEM)
    return pl.pallas_call(
        output_kernel,
        out_shape=jax.ShapeDtypeStruct((rows, cols), BF16),
        in_specs=[vmem] * 3 + [pl.BlockSpec(memory_space=pl.ANY)],
        out_specs=vmem,
        scratch_shapes=[
            VMEM((4, depth, cols), BF16),
            VMEM((3, rows, cols), BF16),
            VMEM((rows, cols), F32),
            VMEM((6, rows // 2, cols), BF16),
            VMEM((2, rows // 2, cols), BF16),
            VMEM((8, rows), F32),
            VMEM((3, 8, rows), F32),
            pltpu.SemaphoreType.DMA((4,)),
            pltpu.SemaphoreType.DMA((6,)),
            pltpu.SemaphoreType.DMA((6,)),
            pltpu.SemaphoreType.DMA((3,)),
            pltpu.SemaphoreType.DMA((3,)),
        ],
        compiler_params=pltpu.CompilerParams(
            collective_id=collective_id, has_side_effects=True, vmem_limit_bytes=40 * 2**20
        ),
        name="output_project",
    )(attended, tokens, gain[None, :], wo)


def window_kernel(count, q_ref, kv_ref, o_ref, tail, acc, lsum, send, recv):
    s = lax.axis_index("seq")
    kv_heads, rows = kv_ref.shape[1], kv_ref.shape[2]
    group = q_ref.shape[0] // kv_heads
    has_next, has_last = s < count - 1, s > 0
    barrier = pltpu.get_barrier_semaphore()

    @pl.when(has_next)
    def _():
        pl.semaphore_signal(barrier, inc=1, device_id={"seq": s + 1}, device_id_type=MESH)

    @pl.when(has_last)
    def _():
        pl.semaphore_signal(barrier, inc=1, device_id={"seq": s - 1}, device_id_type=MESH)

    pl.semaphore_wait(barrier, has_next.astype(jnp.int32) + has_last.astype(jnp.int32))
    copy = remote(
        kv_ref.at[:, :, pl.ds(rows - WINDOW, WINDOW), :], tail, send.at[0], recv.at[0],
        {"seq": s + 1},
    )

    @pl.when(has_next)
    def _():
        copy.start()

    def own(h, carry):
        attend(
            q_ref, kv_ref[0, h], kv_ref[1, h], acc, lsum, h, group,
            lambda row, col: (col <= row) & (row - col < WINDOW), True,
        )
        return carry

    lax.fori_loop(0, kv_heads, own, 0)

    @pl.when(has_last)
    def _():
        copy.wait_recv()

        def body(h, carry):
            attend(
                q_ref, tail[0, h], tail[1, h], acc, lsum, h, group,
                lambda row, col: col > row, False, (0, WINDOW),
            )
            return carry

        lax.fori_loop(0, kv_heads, body, 0)

    write_heads(o_ref, acc, lsum)

    @pl.when(has_next)
    def _():
        copy.wait_send()


def window_attention(q, kv, count, collective_id):
    heads, rows, _ = q.shape
    vmem = pl.BlockSpec(memory_space=VMEM)
    return pl.pallas_call(
        functools.partial(window_kernel, count),
        out_shape=jax.ShapeDtypeStruct((rows, heads * HEAD_DIM), BF16),
        in_specs=[vmem] * 2,
        out_specs=vmem,
        scratch_shapes=[
            VMEM((2, kv.shape[1], WINDOW, HEAD_DIM), BF16),
            VMEM(q.shape, F32),
            VMEM(q.shape, F32),
            pltpu.SemaphoreType.DMA((1,)),
            pltpu.SemaphoreType.DMA((1,)),
        ],
        compiler_params=pltpu.CompilerParams(
            collective_id=collective_id, has_side_effects=True, vmem_limit_bytes=24 * 2**20
        ),
        name="window_attention",
    )(q, kv)


def rms_scaled(values, weights):
    widened = values.astype(F32)
    factor = lax.rsqrt(jnp.mean(widened * widened, axis=-1, keepdims=True) + NORM_EPS)
    return widened * factor * weights


def plain_gather_project(x, gain, cos, sin, wq, wk, wv):
    full = lax.all_gather(x, "tp", axis=1, tiled=True)
    normed = rms_scaled(full, gain).astype(BF16)

    def heads_of(weight):
        product = jnp.dot(normed, weight, preferred_element_type=F32)
        return jnp.swapaxes(product.reshape(x.shape[0], -1, HEAD_DIM), 0, 1)

    def rotated(u):
        return (u * cos + jnp.roll(u, HEAD_DIM // 2, axis=-1) * sin).astype(BF16)

    keys, values = rotated(heads_of(wk)), heads_of(wv).astype(BF16)
    return rotated(heads_of(wq)), jnp.stack([keys, values])


def plain_output_project(attended, tokens, gain, wo):
    cols = tokens.shape[1]
    partial_sum = jnp.dot(attended, wo, preferred_element_type=F32).astype(BF16)
    summed = lax.psum(partial_sum, "tp").astype(F32)
    added = rms_scaled(summed, gain)
    mine = lax.dynamic_slice_in_dim(added, lax.axis_index("tp") * cols, cols, 1)
    return (tokens.astype(F32) + mine).astype(BF16)


def local(
    sizes,
    tokens,
    attention_gain,
    query_weight,
    key_weight,
    value_weight,
    output_weight,
    post_gain,
    local_gain,
    local_query_weight,
    local_key_weight,
    local_value_weight,
):
    seq, tp = sizes
    rows, cols = tokens.shape
    places = lax.axis_index("seq") * rows + lax.iota(jnp.int32, rows)
    halfway = HEAD_DIM // 2
    exponents = jnp.arange(halfway, dtype=F32) * (2.0 / HEAD_DIM)
    frequency = jnp.power(F32(10000.0), -exponents)
    angles = places.astype(F32)[:, None] * frequency[None, :]
    cosine, sine = jnp.cos(angles), jnp.sin(angles)
    cos = jnp.concatenate([cosine, cosine], axis=-1)
    sin = jnp.concatenate([-sine, sine], axis=-1)
    square = tp == 4 and cols % HEAD_DIM == 0

    def project(x, gain, wq, wk, wv, collective_id):
        if square:
            return gather_project(x, gain, cos, sin, wq, wk, wv, collective_id)
        return plain_gather_project(x, gain, cos, sin, wq, wk, wv)

    q, kv = project(tokens, attention_gain, query_weight, key_weight, value_weight, 0)
    attended = causal_attention(q, kv, seq, 1)
    if square:
        hidden = output_project(attended, tokens, post_gain, output_weight, 2)
    else:
        hidden = plain_output_project(attended, tokens, post_gain, output_weight)
    lq, lkv = project(
        hidden, local_gain, local_query_weight, local_key_weight, local_value_weight, 3
    )
    return hidden, window_attention(lq, lkv, seq, 4)


def solution(mesh):
    in_specs = (
        P("seq", "tp"),
        P(),
        P(None, "tp"),
        P(None, "tp"),
        P(None, "tp"),
        P("tp", None),
        P(),
        P(),
        P(None, "tp"),
        P(None, "tp"),
        P(None, "tp"),
    )
    out_specs = (P("seq", "tp"), P("seq", "tp"))
    sizes = (mesh.shape["seq"], mesh.shape["tp"])
    body = functools.partial(local, sizes)
    return jax.shard_map(body, mesh=mesh, in_specs=in_specs, out_specs=out_specs, check_vma=False)
```

time: 260 us -> 136 us (0.52)
  waiting for transfers between devices: 161 us -> 0 us
  Pallas kernels: 0 us -> 130 us
  matrix products: 51.3 us -> 0 us
  other arithmetic: 17.5 us -> 0.69 us
  between operations: 14.8 us -> 0.8 us
  local copies, waits for them, and re-layouts: 12.7 us -> 3.84 us
    pallas_call x0 -> x5, Pallas kernels: none -> 130 us  [the longest x2 54.9 us: gather_project(): pl.pallas_call(functools.partial(gather_project_kernel, heads, kv_heads),...]
    all_gather x3 -> x0, waiting for transfers between devices: 83.5 us -> none  [the longest x1 39 us: local(): full_rows = lax.all_gather(tokens, 'tp', axis=1, tiled=True)]
    psum x1 -> x0, waiting for transfers between devices: 74 us -> none  [local(): lax.psum(jnp.dot(attended, output_weight, preferred_element_type=jnp.floa...]
    dot_general x11 -> x0, matrix products: 51.3 us -> none  [the longest x2 11.7 us: project_heads(): jnp.dot(normed, weight_query, preferred_element_type=jnp.float32)]
    reduce_sum x3 -> x0, other arithmetic: 7.65 us -> none  [rms_scaled(): jnp.mean(widened * widened, axis=-1, keepdims=True) + NORM_EPS]
    and x2 -> x0, other arithmetic: 3.03 us -> none  [the longest x1 2.17 us: attend_block(): allowed = (offset >= 0) & (key_places >= 0)[None, :]]
    another operation x6 -> x0, other arithmetic: 2.95 us -> none
    slice x5 -> x0, local copies, waits for them, and re-layouts: 2.79 us -> none  [the longest x4 2.14 us: rotate(): first_half = vectors[..., :halfway]]
  transfers between devices with their start and end apart: 5 -> 0, of which waited for: 5 -> 0; matrix products, arithmetic and copies ran while one was open for 7% -> 0% of each run, Pallas kernels for 0% -> 0%
where the time goes in v1:
time: 136 us
  Pallas kernels  130 us (96%)
  local copies, waits for them, and re-layouts  3.84 us (3%)
    pallas_call x2, Pallas kernels, gather_project(): pl.pallas_call(functools.partial(gather_project_kernel, heads, kv_heads),...  54.9 us
    pallas_call x1, Pallas kernels, causal_attention(): pl.pallas_call(functools.partial(causal_kernel, count // 2), out_shape=ja...  39.5 us
    pallas_call x1, Pallas kernels, output_project(): pl.pallas_call(output_kernel, out_shape=jax.ShapeDtypeStruct((rows, cols)...  28.4 us
    pallas_call x1, Pallas kernels, window_attention(): pl.pallas_call(functools.partial(window_kernel, count), out_shape=jax.Sha...  7.48 us
    unnamed x16, local copies, waits for them, and re-layouts  2.92 us

profile of v1, /device:TPU:24, one launch (start us, length us, event | category | flops | bytes accessed | tf_op | source)
XLA Modules:
  0.0 135.6 jit_solution(11490402870778101247)
XLA Ops:
  0.7 0.5 fusion
  1.2 0.1 pad_maximum_fusion
  1.3 0.0 slice-start
  1.4 0.9 broadcast_in_dim.11.gain_ref
  2.3 0.0 copy-start
  2.3 1.3 copy-done
  3.5 0.0 copy-start.2
  3.5 0.0 slice-start.1
  3.5 0.0 slice-start.2
  3.5 0.0 copy-start.1
  3.6 27.9 %gather_project_0.1 = (bf16[8,256,128]{2,1,0:T(8,128)(2,1)S(1)}, bf16[2,4,256,128]{3,2,1,0:T(8,128)(2,1)S(1)}) custom-call(bf16[256,1152]{1,0:T(8,128)(2,1)S(1)} %copy-done, f32[1,4608]{1,0:T(1,128)S(1)} %broadcast_in_dim.11.gain_ref, f32[256,128]{1,0:T(8,128)S(1)} %get-tuple-element.13.cos_ref, f32[256,128]{1,0:T(8,128)S(1)} %get-tuple-element.14.sin_ref, ...), custom_call_target="tpu_custom_call" | custom-call | tf_op jit(solution)/shard_map/gather_project_0/pallas_call | solution.py:159
  31.5 39.5 %causal_attention.1.a_ref = bf16[256,1024]{1,0:T(8,128)(2,1)S(1)} custom-call(bf16[8,256,128]{2,1,0:T(8,128)(2,1)S(1)} %get-tuple-element.6.q_ref, bf16[2,4,256,128]{3,2,1,0:T(8,128)(2,1)S(1)} %get-tuple-element.7.kv_ref), custom_call_target="tpu_custom_call" | custom-call | tf_op jit(solution)/shard_map/causal_attention/pallas_call | solution.py:321
  71.0 0.0 copy-done.2
  71.1 0.0 slice-done
  71.1 0.0 slice-done.1
  71.1 0.0 slice-done.2
  71.1 0.0 copy-done.1
  71.1 0.0 copy-start.3
  71.1 28.4 %output_project.1.x_ref = bf16[256,1152]{1,0:T(8,128)(2,1)S(1)} custom-call(bf16[256,1024]{1,0:T(8,128)(2,1)S(1)} %causal_attention.1.a_ref, bf16[256,1152]{1,0:T(8,128)(2,1)S(1)} %copy-done.1, f32[1,4608]{1,0:T(1,128)S(1)} %broadcast_in_dim.12.gain_ref, bf16[1024,4608]{1,0:T(8,128)(2,1)S(1)} %bitcast.1), custom_call_target="tpu_custom_call" | custom-call | tf_op jit(solution)/shard_map/output_project/pallas_call | solution.py:447
  99.5 0.0 copy-done.3
  99.5 26.9 %gather_project_3.1 = (bf16[8,256,128]{2,1,0:T(8,128)(2,1)S(1)}, bf16[2,4,256,128]{3,2,1,0:T(8,128)(2,1)S(1)}) custom-call(bf16[256,1152]{1,0:T(8,128)(2,1)S(1)} %output_project.1.x_ref, f32[1,4608]{1,0:T(1,128)S(1)} %broadcast_in_dim.13.gain_ref, f32[256,128]{1,0:T(8,128)S(1)} %get-tuple-element.13.cos_ref, f32[256,128]{1,0:T(8,128)S(1)} %get-tuple-element.14.sin_ref, ...), custom_call_target="tpu_custom_call" | custom-call | tf_op jit(solution)/shard_map/gather_project_3/pallas_call | solution.py:159
  126.5 7.5 %window_attention.1 = bf16[256,1024]{1,0:T(8,128)(2,1)S(1)} custom-call(bf16[8,256,128]{2,1,0:T(8,128)(2,1)S(1)} %get-tuple-element.8.q_ref, bf16[2,4,256,128]{3,2,1,0:T(8,128)(2,1)S(1)} %get-tuple-element.9.kv_ref), custom_call_target="tpu_custom_call" | custom-call | tf_op jit(solution)/shard_map/window_attention/pallas_call | solution.py:530
  134.0 0.8 copy.15
  134.8 0.8 copy.16
  (5 shorter events, 0.0 us)
Async XLA Ops:
  1.3 69.7 %slice-start = ((s8[9437184]{0:T(1024)(128)(4,1)}), s8[4194304]{0:T(1024)(128)(4,1)S(1)}, s32[]{:S(2)}) async-start(s8[9437184]{0:T(1024)(128)(4,1)} %bitcast), calls=%async_computation | async-start | bytes 8388608
  2.3 1.3 copy-start
  3.5 67.5 %copy-start.2 = (f32[4608]{0:T(1024)S(1)}, f32[4608]{0:T(1024)}, u32[]{:S(2)}) copy-start(f32[4608]{0:T(1024)} %param.17) | copy-start | bytes 55300
  3.5 67.5 %slice-start.1 = ((s8[9437184]{0:T(1024)(128)(4,1)}), s8[4194304]{0:T(1024)(128)(4,1)S(1)}, s32[]{:S(2)}) async-start(s8[9437184]{0:T(1024)(128)(4,1)} %bitcast), calls=%async_computation.1 | async-start | bytes 8388608
  3.5 67.5 %slice-start.2 = ((s8[9437184]{0:T(1024)(128)(4,1)}), s8[1048576]{0:T(1024)(128)(4,1)S(1)}, s32[]{:S(2)}) async-start(s8[9437184]{0:T(1024)(128)(4,1)} %bitcast), calls=%async_computation.2 | async-start | bytes 2097152
  3.5 67.6 %copy-start.1 = (bf16[256,1152]{1,0:T(8,128)(2,1)S(1)}, bf16[256,1152]{1,0:T(8,128)(2,1)}, u32[]{:S(2)}) copy-start(bf16[256,1152]{1,0:T(8,128)(2,1)} %tok_ref.1) | copy-start | bytes 1769476
  71.1 28.4 %copy-start.3 = (f32[4608]{0:T(1024)S(1)}, f32[4608]{0:T(1024)}, u32[]{:S(2)}) copy-start(f32[4608]{0:T(1024)} %param.18) | copy-start | bytes 55300

commit v2 on v1

--- a/solution.py
+++ b/solution.py
@@ -336,6 +336,300 @@
         ),
         name="causal_attention",
     )(q, kv)
+
+
+def front_kernel(
+    levels, heads, kv_heads, x_ref, gain_ref, cos_ref, sin_ref, wq_ref, wk_ref, wv_ref,
+    o_ref, buf, xg, w, acc, ss, q_all, kv_own, kv_buf, out, lsum,
+    send, recv, wsem, up_sem, side_sem, kv_sem,
+):
+    me = lax.axis_index("tp")
+    s = lax.axis_index("seq")
+    z, c = s // 2, s % 2
+    mate = s + 1 - 2 * c
+    has_up, has_down = z < levels - 1, z > 0
+    rows, cols = x_ref.shape
+    half, quarter = rows // 2, rows // 4
+    owners = [xor(me, bits) for bits in range(4)]
+    along_x, along_y = {"tp": owners[1]}, {"tp": owners[2]}
+    qc, kc = heads * HEAD_DIM, kv_heads * HEAD_DIM
+    total = qc + 2 * kc
+    group = heads // kv_heads
+
+    loads = []
+    for slot in range(4):
+        span = pl.ds(pl.multiple_of(owners[slot] * cols, cols), cols)
+        parts = ((wq_ref, 0, qc), (wk_ref, qc, kc), (wv_ref, qc + kc, kc))
+        bundle = []
+        for which, (ref, begin, width) in enumerate(parts):
+            copy = pltpu.make_async_copy(
+                ref.at[span, :], w.at[slot, :, pl.ds(begin, width)], wsem.at[slot, which]
+            )
+            copy.start()
+            bundle.append(copy)
+        loads.append(bundle)
+
+    barrier = pltpu.get_barrier_semaphore()
+    for peer in (along_x, along_y, {"seq": mate}):
+        pl.semaphore_signal(barrier, inc=1, device_id=peer, device_id_type=MESH)
+
+    @pl.when(has_up)
+    def _():
+        pl.semaphore_signal(barrier, inc=1, device_id={"seq": s + 2}, device_id_type=MESH)
+
+    @pl.when(has_down)
+    def _():
+        pl.semaphore_signal(barrier, inc=1, device_id={"seq": s - 2}, device_id_type=MESH)
+
+    pl.semaphore_wait(barrier, 3 + has_up.astype(jnp.int32) + has_down.astype(jnp.int32))
+
+    moves = []
+    for part in range(2):
+        top, bottom = pl.ds(part * half, quarter), pl.ds(part * half + quarter, quarter)
+        spec = (
+            (x_ref.at[top], buf.at[0, top], along_x),
+            (x_ref.at[bottom], buf.at[1, bottom], along_y),
+            (x_ref.at[bottom], buf.at[0, bottom], along_x),
+            (x_ref.at[top], buf.at[1, top], along_y),
+            (buf.at[0, top], buf.at[2, top], along_y),
+            (buf.at[1, bottom], buf.at[2, bottom], along_x),
+        )
+        moves.append(
+            [
+                remote(source, target, send.at[part * 6 + i], recv.at[part * 6 + i], device)
+                for i, (source, target, device) in enumerate(spec)
+            ]
+        )
+
+    def begin_gather(part):
+        for i in range(4):
+            moves[part][i].start()
+
+    def pass_on(part):
+        moves[part][0].wait_recv()
+        moves[part][4].start()
+        moves[part][1].wait_recv()
+        moves[part][5].start()
+
+    def up(owner, part, source):
+        index = owner * 2 + part
+        return remote(
+            source, kv_buf.at[index], up_sem.at[index], kv_sem.at[index], {"seq": s + 2}
+        )
+
+    def side(owner, part, source):
+        index = owner * 2 + part
+        return remote(
+            source, kv_buf.at[index], side_sem.at[index], kv_sem.at[index], {"seq": mate}
+        )
+
+    def arrive(owner, part):
+        block = kv_buf.at[owner * 2 + part]
+        up(owner, part, block).wait_recv()
+
+        @pl.when(has_up)
+        def _():
+            up(owner, part, block).start()
+
+        side(owner, part, block).start()
+
+    tile = 256 if total % 256 == 0 else 128
+    step_rows = 64 if half % 64 == 0 else half
+
+    def take(slot, part, source):
+        gain_span = pl.ds(pl.multiple_of(owners[slot] * cols, cols), cols)
+
+        def prepare(i, carry):
+            here = pl.ds(pl.multiple_of(i * step_rows, step_rows), step_rows)
+            there = pl.ds(pl.multiple_of(part * half + i * step_rows, step_rows), step_rows)
+            wide = source[there, :].astype(F32)
+            squares = jnp.sum(wide * wide, axis=-1, keepdims=True)
+            spread = jnp.broadcast_to(squares, (step_rows, HEAD_DIM))
+            if slot == 0:
+                ss[here, :] = spread
+            else:
+                ss[here, :] += spread
+            xg[here, :] = (wide * gain_ref[:, gain_span]).astype(BF16)
+            return carry
+
+        lax.fori_loop(0, half // step_rows, prepare, 0)
+        if part == 0:
+            for copy in loads[slot]:
+                copy.wait()
+
+        def multiply(j, carry):
+            span = pl.ds(pl.multiple_of(j * tile, tile), tile)
+            product = jnp.dot(xg[...], w[slot, :, span], preferred_element_type=F32)
+            if slot == 0:
+                acc[:, span] = product
+            else:
+                acc[:, span] += product
+            return carry
+
+        lax.fori_loop(0, total // tile, multiply, 0)
+
+    def finish_part(part):
+        factor = lax.rsqrt(ss[...] * (1.0 / D) + NORM_EPS)
+        span = pl.ds(part * half, half)
+
+        def rotated(index):
+            u = acc[:, pl.ds(index * HEAD_DIM, HEAD_DIM)] * factor
+            turned = pltpu.roll(u, HEAD_DIM // 2, 1)
+            return (u * cos_ref[span, :] + turned * sin_ref[span, :]).astype(BF16)
+
+        for h in range(kv_heads):
+            kv_own[part, 0, h] = rotated(heads + h)
+            place = (heads + kv_heads + h) * HEAD_DIM
+            kv_own[part, 1, h] = (acc[:, pl.ds(place, HEAD_DIM)] * factor).astype(BF16)
+        for h in range(heads):
+            q_all[h, span] = rotated(h)
+
+        @pl.when(has_up)
+        def _():
+            up(s, part, kv_own.at[part]).start()
+
+        @pl.when(c == 0)
+        def _():
+            side(s, part, kv_own.at[part]).start()
+
+    begin_gather(0)
+    take(0, 0, x_ref)
+    pass_on(0)
+    begin_gather(1)
+    moves[0][2].wait_recv()
+    take(1, 0, buf.at[0])
+    moves[0][3].wait_recv()
+    take(2, 0, buf.at[1])
+    moves[0][4].wait_recv()
+    moves[0][5].wait_recv()
+    take(3, 0, buf.at[2])
+    finish_part(0)
+    pass_on(1)
+    take(0, 1, x_ref)
+    moves[1][2].wait_recv()
+    take(1, 1, buf.at[0])
+    moves[1][3].wait_recv()
+    take(2, 1, buf.at[1])
+
+    @pl.when(has_down)
+    def _():
+        arrive(s - 2, 0)
+
+    moves[1][4].wait_recv()
+    moves[1][5].wait_recv()
+    take(3, 1, buf.at[2])
+    finish_part(1)
+
+    for part in range(2):
+        shift = part * half
+
+        def own(h, carry):
+            attend(
+                q_all, kv_own[part, 0, h], kv_own[part, 1, h], out, lsum, h, group,
+                lambda row, col: col + shift <= row, part == 0,
+            )
+            return carry
+
+        lax.fori_loop(0, kv_heads, own, 0)
+
+    def visit(owner, part):
+        index = owner * 2 + part
+
+        def body(h, carry):
+            attend(
+                q_all, kv_buf[index, 0, h], kv_buf[index, 1, h], out, lsum, h, group, None, False
+            )
+            return carry
+
+        lax.fori_loop(0, kv_heads, body, 0)
+
+    @pl.when(z > 0)
+    def _():
+        arrive(s - 2, 1)
+
+    @pl.when(c == 1)
+    def _():
+        for part in range(2):
+            side(s - 1, part, kv_buf.at[(s - 1) * 2 + part]).wait_recv()
+            visit(s - 1, part)
+
+    def level(unit, carry):
+        k, part = 1 + unit // 2, unit % 2
+        owner, other = s - 2 * k, mate - 2 * k
+
+        @pl.when(unit >= 2)
+        def _():
+            arrive(owner, part)
+
+        visit(owner, part)
+        side(other, part, kv_buf.at[other * 2 + part]).wait_recv()
+        visit(other, part)
+        return carry
+
+    lax.fori_loop(0, 2 * z, level, 0)
+    write_heads(o_ref, out, lsum)
+
+    for part in range(2):
+        for copy in moves[part]:
+            copy.wait_send()
+
+        @pl.when(has_up)
+        def _():
+            up(s, part, kv_own.at[part]).wait_send()
+
+        @pl.when(c == 0)
+        def _():
+            side(s, part, kv_own.at[part]).wait_send()
+
+    def drain(unit, carry):
+        owner, part = s - 2 * (1 + unit // 2), unit % 2
+        block = kv_buf.at[owner * 2 + part]
+
+        @pl.when(has_up)
+        def _():
+            up(owner, part, block).wait_send()
+
+        side(owner, part, block).wait_send()
+        return carry
+
+    lax.fori_loop(0, 2 * z, drain, 0)
+
+
+def front(x, gain, cos, sin, wq, wk, wv, count, collective_id):
+    rows, cols = x.shape
+    half = rows // 2
+    heads, kv_heads = wq.shape[1] // HEAD_DIM, wk.shape[1] // HEAD_DIM
+    total = wq.shape[1] + 2 * wk.shape[1]
+    vmem = pl.BlockSpec(memory_space=VMEM)
+    hbm = pl.BlockSpec(memory_space=pl.ANY)
+    return pl.pallas_call(
+        functools.partial(front_kernel, count // 2, heads, kv_heads),
+        out_shape=jax.ShapeDtypeStruct((rows, heads * HEAD_DIM), BF16),
+        in_specs=[vmem] * 4 + [hbm] * 3,
+        out_specs=vmem,
+        scratch_shapes=[
+            VMEM((3, rows, cols), BF16),
+            VMEM((half, cols), BF16),
+            VMEM((4, cols, total), BF16),
+            VMEM((half, total), F32),
+            VMEM((half, HEAD_DIM), F32),
+            VMEM((heads, rows, HEAD_DIM), BF16),
+            VMEM((2, 2, kv_heads, half, HEAD_DIM), BF16),
+            VMEM((2 * count, 2, kv_heads, half, HEAD_DIM), BF16),
+            VMEM((heads, rows, HEAD_DIM), F32),
+            VMEM((heads, rows, HEAD_DIM), F32),
+            pltpu.SemaphoreType.DMA((12,)),
+            pltpu.SemaphoreType.DMA((12,)),
+            pltpu.SemaphoreType.DMA((4, 3)),
+            pltpu.SemaphoreType.DMA((2 * count,)),
+            pltpu.SemaphoreType.DMA((2 * count,)),
+            pltpu.SemaphoreType.DMA((2 * count,)),
+        ],
+        compiler_params=pltpu.CompilerParams(
+            collective_id=collective_id, has_side_effects=True, vmem_limit_bytes=48 * 2**20
+        ),
+        name="front",
+    )(x, gain[None, :], cos, sin, wq, wk, wv)
 
 
 def output_kernel(
@@ -607,11 +901,12 @@
             return gather_project(x, gain, cos, sin, wq, wk, wv, collective_id)
         return plain_gather_project(x, gain, cos, sin, wq, wk, wv)
 
-    q, kv = project(tokens, attention_gain, query_weight, key_weight, value_weight, 0)
-    attended = causal_attention(q, kv, seq, 1)
+    first = (tokens, attention_gain, cos, sin, query_weight, key_weight, value_weight)
     if square:
+        attended = front(*first, seq, 0)
         hidden = output_project(attended, tokens, post_gain, output_weight, 2)
     else:
+        attended = causal_attention(*plain_gather_project(*first), seq, 1)
         hidden = plain_output_project(attended, tokens, post_gain, output_weight)
     lq, lkv = project(
         hidden, local_gain, local_query_weight, local_key_weight, local_value_weight, 3

time: 136 us -> 131 us (0.963)
  Pallas kernels: 130 us -> 123 us
  local copies, waits for them, and re-layouts: 3.84 us -> 6.18 us
    pallas_call x2 -> x1, Pallas kernels: 54.9 us -> 26.9 us  [gather_project(): pl.pallas_call(functools.partial(gather_project_kernel, heads, kv_heads),...]
    pallas_call x1, Pallas kernels: 39.5 us -> 59.6 us  [front(): pl.pallas_call(functools.partial(front_kernel, count // 2, heads, kv_head...]
    unnamed x16 -> x18, local copies, waits for them, and re-layouts: 2.92 us -> 5.26 us
where the time goes in v2:
time: 131 us
  Pallas kernels  123 us (94%)
  local copies, waits for them, and re-layouts  6.18 us (5%)
    pallas_call x1, Pallas kernels, front(): pl.pallas_call(functools.partial(front_kernel, count // 2, heads, kv_head...  59.6 us
    pallas_call x1, Pallas kernels, output_project(): pl.pallas_call(output_kernel, out_shape=jax.ShapeDtypeStruct((rows, cols)...  29.1 us
    pallas_call x1, Pallas kernels, gather_project(): pl.pallas_call(functools.partial(gather_project_kernel, heads, kv_heads),...  26.9 us
    pallas_call x1, Pallas kernels, window_attention(): pl.pallas_call(functools.partial(window_kernel, count), out_shape=jax.Sha...  7.48 us
    unnamed x18, local copies, waits for them, and re-layouts  5.26 us

profile of v2, /device:TPU:24, one launch (start us, length us, event | category | flops | bytes accessed | tf_op | source)
XLA Modules:
  0.0 130.8 jit_solution(11204726682055730003)
XLA Ops:
  0.7 0.5 fusion
  1.2 0.0 slice-start
  1.2 0.1 pad_maximum_fusion
  1.4 0.9 broadcast_in_dim.11.gain_ref
  2.3 0.0 copy-start
  2.3 2.6 %copy-done = bf16[4608,512]{1,0:T(8,128)(2,1)S(1)} copy-done((bf16[4608,512]{1,0:T(8,128)(2,1)S(1)}, bf16[4608,512]{1,0:T(8,128)(2,1)}, u32[]{:S(2)}) %copy-start) | copy-done | bytes 4718616
  4.8 0.0 copy-start.1
  4.8 1.1 copy-done.1
  5.9 0.0 copy-start.3
  5.9 0.0 slice-start.1
  5.9 0.0 slice-start.2
  5.9 0.0 copy-start.2
  5.9 59.6 %front.1.a_ref = bf16[256,1024]{1,0:T(8,128)(2,1)S(1)} custom-call(bf16[256,1152]{1,0:T(8,128)(2,1)S(1)} %copy-done.1, f32[1,4608]{1,0:T(1,128)S(1)} %broadcast_in_dim.11.gain_ref, f32[256,128]{1,0:T(8,128)S(1)} %get-tuple-element.9.cos_ref, f32[256,128]{1,0:T(8,128)S(1)} %get-tuple-element.10.sin_ref, bf16[4608,1024]{1,0:T(8,128)(2,1)} %wq_ref.2, ...), custom_call_target="tpu_custom_call" | custom-call | tf_op jit(solution)/shard_map/front/pallas_call | solution.py:605
  65.5 0.0 copy-done.3
  65.6 0.0 slice-done
  65.6 0.0 slice-done.1
  65.6 0.0 slice-done.2
  65.6 0.0 copy-done.2
  65.6 0.0 copy-start.4
  65.6 29.1 %output_project.1.x_ref = bf16[256,1152]{1,0:T(8,128)(2,1)S(1)} custom-call(bf16[256,1024]{1,0:T(8,128)(2,1)S(1)} %front.1.a_ref, bf16[256,1152]{1,0:T(8,128)(2,1)S(1)} %copy-done.2, f32[1,4608]{1,0:T(1,128)S(1)} %broadcast_in_dim.12.gain_ref, bf16[1024,4608]{1,0:T(8,128)(2,1)S(1)} %bitcast.1), custom_call_target="tpu_custom_call" | custom-call | tf_op jit(solution)/shard_map/output_project/pallas_call | solution.py:741
  94.8 0.0 copy-done.4
  94.8 26.9 %gather_project_3.1 = (bf16[8,256,128]{2,1,0:T(8,128)(2,1)S(1)}, bf16[2,4,256,128]{3,2,1,0:T(8,128)(2,1)S(1)}) custom-call(bf16[256,1152]{1,0:T(8,128)(2,1)S(1)} %output_project.1.x_ref, f32[1,4608]{1,0:T(1,128)S(1)} %broadcast_in_dim.13.gain_ref, f32[256,128]{1,0:T(8,128)S(1)} %get-tuple-element.9.cos_ref, f32[256,128]{1,0:T(8,128)S(1)} %get-tuple-element.10.sin_ref, ...), custom_call_target="tpu_custom_call" | custom-call | tf_op jit(solution)/shard_map/gather_project_3/pallas_call | solution.py:159
  121.8 7.5 %window_attention.1 = bf16[256,1024]{1,0:T(8,128)(2,1)S(1)} custom-call(bf16[8,256,128]{2,1,0:T(8,128)(2,1)S(1)} %get-tuple-element.4.q_ref, bf16[2,4,256,128]{3,2,1,0:T(8,128)(2,1)S(1)} %get-tuple-element.5.kv_ref), custom_call_target="tpu_custom_call" | custom-call | tf_op jit(solution)/shard_map/window_attention/pallas_call | solution.py:824
  129.2 0.8 copy.15
  130.1 0.8 copy.16
  (5 shorter events, 0.0 us)
Async XLA Ops:
  1.2 64.4 %slice-start = ((s8[9437184]{0:T(1024)(128)(4,1)}), s8[4194304]{0:T(1024)(128)(4,1)S(1)}, s32[]{:S(2)}) async-start(s8[9437184]{0:T(1024)(128)(4,1)} %bitcast), calls=%async_computation | async-start | bytes 8388608
  2.3 2.6 %copy-start = (bf16[4608,512]{1,0:T(8,128)(2,1)S(1)}, bf16[4608,512]{1,0:T(8,128)(2,1)}, u32[]{:S(2)}) copy-start(bf16[4608,512]{1,0:T(8,128)(2,1)} %wk_ref.2) | copy-start | bytes 14155780
  4.8 1.1 copy-start.1
  5.9 59.7 %copy-start.3 = (f32[4608]{0:T(1024)S(1)}, f32[4608]{0:T(1024)}, u32[]{:S(2)}) copy-start(f32[4608]{0:T(1024)} %param.17) | copy-start | bytes 55300
  5.9 59.7 %slice-start.1 = ((s8[9437184]{0:T(1024)(128)(4,1)}), s8[4194304]{0:T(1024)(128)(4,1)S(1)}, s32[]{:S(2)}) async-start(s8[9437184]{0:T(1024)(128)(4,1)} %bitcast), calls=%async_computation.1 | async-start | bytes 8388608
  5.9 59.7 %slice-start.2 = ((s8[9437184]{0:T(1024)(128)(4,1)}), s8[1048576]{0:T(1024)(128)(4,1)S(1)}, s32[]{:S(2)}) async-start(s8[9437184]{0:T(1024)(128)(4,1)} %bitcast), calls=%async_computation.2 | async-start | bytes 2097152
  5.9 59.7 %copy-start.2 = (bf16[256,1152]{1,0:T(8,128)(2,1)S(1)}, bf16[256,1152]{1,0:T(8,128)(2,1)}, u32[]{:S(2)}) copy-start(bf16[256,1152]{1,0:T(8,128)(2,1)} %tok_ref.1) | copy-start | bytes 1769476
  65.6 29.2 %copy-start.4 = (f32[4608]{0:T(1024)S(1)}, f32[4608]{0:T(1024)}, u32[]{:S(2)}) copy-start(f32[4608]{0:T(1024)} %param.18) | copy-start | bytes 55300
